TPU v7x, 32 devices: a whole 2x2x4 slice. The times are simulated.
32 devices in a mesh: kx: 8 (over z, x), cz: 4 (over y, core).
Axes of the slice: x: 2, y: 2, z: 4, core: 2. Of those that a mesh axis runs over, the one named last changes fastest.
Arguments:
- field_modes: bfloat16 [512, 4, 12288], P('cz', None, 'kx'), may hold values from -6 to 6
- cotangent: bfloat16 [512, 4, 12288], P('cz', None, 'kx'), may hold values from -6 to 6
Outputs:
- mode_gradient: bfloat16 [512, 4, 12288], P('cz', None, 'kx')
All inputs are finite; a program needn't handle non-finite values.
Results may differ from a plain program's by a relative error of at most 0.009.
Values may be sent and summed in bfloat16 or wider, within the bound.
A program may use at most 128 MiB of HBM per device.

v0:
```python
import math

import jax
import jax.numpy as jnp
from jax import lax
from jax.sharding import PartitionSpec as P

NZ = 512
MZ = 768
NX = 768
Y = 16


def cosine_table():
    row_index = jnp.arange(MZ, dtype=jnp.int32)
    col_index = jnp.arange(NZ, dtype=jnp.int32)
    position = col_index[None, :] * (2 * row_index[:, None] + 1) % (4 * MZ)
    return jnp.cos(jnp.pi * position.astype(jnp.float32) / (2 * MZ))


def hartley_table():
    points = jnp.arange(NX, dtype=jnp.int32)
    position = points[:, None] * points[None, :] % NX
    phases = 2.0 * jnp.pi * position.astype(jnp.float32) / NX
    return ((jnp.cos(phases) + jnp.sin(phases)) / math.sqrt(NX)).astype(jnp.bfloat16)


def product_gradient(fields, adjoint):
    vertical = fields[2]
    return jnp.stack(
        [
            adjoint[0] * vertical,
            adjoint[1] * vertical,
            adjoint[0] * fields[0]
            + adjoint[1] * fields[1]
            + 2.0 * adjoint[2] * vertical
            + adjoint[3] * fields[3],
            adjoint[3] * vertical,
        ]
    ).astype(jnp.bfloat16)


def on_device(field_modes, cotangent):
    local_modes = field_modes.shape[0]
    field_count = field_modes.shape[1]
    local_columns = field_modes.shape[2] // Y
    field_grid = field_modes.reshape(local_modes, field_count, local_columns, Y)
    cotangent_grid = cotangent.reshape(local_modes, field_count, local_columns, Y)
    cosines = cosine_table()
    synthesis = (cosines * math.sqrt(2.0 / NZ)).astype(jnp.bfloat16)
    projection = (cosines * math.sqrt(2.0 / MZ)).astype(jnp.bfloat16)
    hartley = hartley_table()
    lifted = jnp.concatenate(
        [
            jnp.einsum(
                "zk,kfxy->yfxz",
                synthesis,
                lax.all_to_all(field_grid, "cz", split_axis=3, concat_axis=0, tiled=True),
                preferred_element_type=jnp.float32,
            ).astype(jnp.bfloat16),
            jnp.einsum(
                "zk,kfxy->yfxz",
                projection,
                lax.all_to_all(cotangent_grid, "cz", split_axis=3, concat_axis=0, tiled=True),
                preferred_element_type=jnp.float32,
            ).astype(jnp.bfloat16),
        ],
        axis=1,
    )
    piece = lax.all_to_all(lifted, "kx", split_axis=3, concat_axis=2, tiled=True)
    fields = jnp.einsum(
        "xm,yfmz->fyzx", hartley, piece[:, :field_count], preferred_element_type=jnp.float32
    )
    adjoint = jnp.einsum(
        "xm,yfmz->fyzx", hartley, piece[:, field_count:], preferred_element_type=jnp.float32
    )
    gradient = product_gradient(fields, adjoint)
    turned = jnp.einsum(
        "xm,fyzx->yfmz", hartley, gradient, preferred_element_type=jnp.float32
    ).astype(jnp.bfloat16)
    returned = lax.all_to_all(turned, "kx", split_axis=2, concat_axis=3, tiled=True)
    spectral = jnp.einsum(
        "zk,yfxz->kfxy", synthesis, returned, preferred_element_type=jnp.float32
    ).astype(jnp.bfloat16)
    result = lax.all_to_all(spectral, "cz", split_axis=0, concat_axis=3, tiled=True)
    return result.reshape(local_modes, field_count, local_columns * Y)


def solution(mesh):
    return jax.shard_map(
        on_device,
        mesh=mesh,
        in_specs=(P("cz", None, "kx"), P("cz", None, "kx")),
        out_specs=P("cz", None, "kx"),
        check_vma=False,
    )
```

profile of v0, /device:TPU:0, one launch (start us, length us, event | category | flops | bytes accessed | tf_op | source)
XLA Modules:
  0.0 435.8 jit_solution(16268019331299790281)
XLA Ops:
  0.0 3.0 copy.18
  3.0 1.6 copy.19
  4.5 4.3 all-to-all-start
  8.8 3.0 copy.22
  11.7 1.6 copy.23
  13.3 15.5 %all-to-all-done = bf16[128,4,96,16]{0,2,1,3:T(8,128)(2,1)S(1)} async-done(((bf16[128,4,96,16]{0,2,1,3:T(8,128)(2,1)}), bf16[128,4,96,16]{0,2,1,3:T(8,128)(2,1)S(1)}, u32[]{:S(2)}, u32[]{:S(2)}) %all-to-all-start) | async-done | bytes 1572896 | tf_op jit(solution)/shard_map/all_to_all | solution.py:58
  28.8 3.6 all-to-all-start.1
  32.4 2.4 copy.21
  34.8 3.6 all_to_all.66
  38.4 14.0 %all-to-all-done.1 = bf16[128,4,96,16]{0,2,1,3:T(8,128)(2,1)S(1)} async-done(((bf16[128,4,96,16]{0,2,1,3:T(8,128)(2,1)}), bf16[128,4,96,16]{0,2,1,3:T(8,128)(2,1)S(1)}, u32[]{:S(2)}, u32[]{:S(2)}) %all-to-all-start.1) | async-done | bytes 1572896 | tf_op jit(solution)/shard_map/all_to_all | solution.py:64
  52.4 1.2 copy.25
  53.6 2.0 all_to_all.70
  55.6 9.7 %convert_bitcast_fusion.2 = bf16[4,4,96,768]{3,2,0,1:T(8,128)(2,1)S(1)} fusion(bf16[512,4,96,4]{0,2,3,1:T(8,128)(2,1)S(1)} %copy-done.1, s32[768]{0:T(1024)S(1)} %multiply_add_fusion), kind=kOutput, calls=%fused_computation.16 | convolution fusion | flops 1213464576 | bytes 3935232 | tf_op jit(solution)/shard_map/zk,kfxy->yfxz/dot_general | solution.py:55
  65.4 9.7 %convert_bitcast_fusion.1 = bf16[4,4,96,768]{3,2,0,1:T(8,128)(2,1)S(1)} fusion(bf16[512,4,96,4]{0,2,3,1:T(8,128)(2,1)S(1)} %copy-done.2, s32[768]{0:T(1024)S(1)} %multiply_add_fusion), kind=kOutput, calls=%fused_computation.15 | convolution fusion | flops 1213464576 | bytes 3935232 | tf_op jit(solution)/shard_map/zk,kfxy->yfxz/dot_general | solution.py:61
  75.1 2.6 pad_maximum_fusion
  77.7 10.9 %copy.26 = bf16[4,8,96,768]{2,0,1,3:T(4,128)(2,1)} copy(bf16[4,8,96,768]{3,2,0,1:T(8,128)(2,1)} %pad_maximum_fusion) | data formatting | bytes 9437184 | tf_op jit(solution)/shard_map/concatenate | solution.py:53
  88.7 144.9 %all_to_all.87 = bf16[4,8,96,768]{2,0,1,3:T(4,128)(2,1)S(1)} all-to-all(bf16[4,8,96,768]{2,0,1,3:T(4,128)(2,1)} %copy.26), channel_id=1, replica_groups=mesh['kx'=8,'cz'=4] {'kx'}, dimensions={3} | all-to-all | bytes 9437184 | tf_op jit(solution)/shard_map/all_to_all | solution.py:70
  233.6 6.7 %copy.45 = bf16[4,8,96,8,96]{2,3,4,1,0:T(8,128)(2,1)} copy(bf16[4,8,96,8,96]{2,0,1,4,3:T(4,128)(2,1)S(1)} %bitcast.65) | data formatting | bytes 9437184 | tf_op jit(solution)/shard_map/all_to_all | solution.py:70
  240.3 10.8 %all_to_all.74 = bf16[4,8,768,96]{2,3,1,0:T(8,128)(2,1)} reshape(bf16[4,8,8,96,96]{3,2,4,1,0:T(8,128)(2,1)} %bitcast.66) | data formatting | bytes 9437184 | tf_op jit(solution)/shard_map/all_to_all | solution.py:70
  251.1 12.7 %convolution_bitcast_fusion = f32[4,4,96,768]{3,2,0,1:T(8,128)S(1)} fusion(bf16[4,8,768,96]{2,3,1,0:T(8,128)(2,1)} %all_to_all.74), kind=kOutput, calls=%fused_computation.18 | convolution fusion | flops 1819017216 | bytes 9437184 | tf_op jit(solution)/shard_map/xm,yfmz->fyzx/dot_general | solution.py:71
  263.8 25.5 %convolution_bitcast_fusion.1 = f32[4,4,96,768]{3,2,0,1:T(8,128)S(1)} fusion(bf16[4,8,768,96]{2,3,1,0:T(8,128)(2,1)S(1)} %copy-done), kind=kOutput, calls=%fused_computation.19 | convolution fusion | flops 1819017216 | bytes 9437184 | tf_op jit(solution)/shard_map/xm,yfmz->fyzx/dot_general | solution.py:74
  289.3 0.9 multiply_convert_fusion.5
  290.2 12.3 %convert_bitcast_fusion = bf16[4,4,768,96]{2,3,0,1:T(8,128)(2,1)} fusion(bf16[1,4,96,768]{3,2,0,1:T(8,128)(2,1)S(1)} %get-tuple-element.6, bf16[1,4,96,768]{3,2,0,1:T(8,128)(2,1)S(1)} %get-tuple-element.7, bf16[1,4,96,768]{3,2,0,1:T(8,128)(2,1)S(1)} %get-tuple-element.8, bf16[1,4,96,768]{3,2,0,1:T(8,128)(2,1)S(1)} %get-tuple-element.5), kind=kOutput, calls=%fused_computation.10 | convolution fusion | flops 1823735808 | bytes 4718592 | tf_op jit(solution)/shard_map/xm,fyzx->yfmz/dot_general | solution.py:78
  302.5 5.0 %copy.29 = bf16[4,4,768,96]{3,0,1,2:T(4,128)(2,1)S(1)} copy(bf16[4,4,768,96]{2,3,0,1:T(8,128)(2,1)} %convert_bitcast_fusion) | data formatting | bytes 4718592 | tf_op jit(solution)/shard_map/convert_element_type | solution.py:80
  307.5 73.6 %all_to_all.88 = bf16[4,4,768,96]{3,0,1,2:T(4,128)(2,1)S(1)} all-to-all(bf16[4,4,768,96]{3,0,1,2:T(4,128)(2,1)S(1)} %copy.29), channel_id=1, replica_groups=mesh['kx'=8,'cz'=4] {'kx'}, dimensions={2} | all-to-all | bytes 4718592 | tf_op jit(solution)/shard_map/all_to_all | solution.py:81
  381.1 2.0 copy.46
  383.1 3.6 all_to_all.78
  386.7 9.9 %fusion.15 = bf16[512,4,96,4]{0,2,1,3:T(8,128)(2,1)} fusion(bf16[4,4,96,768]{3,2,1,0:T(8,128)(2,1)} %all_to_all.78, s32[768]{0:T(1024)S(1)} %multiply_add_fusion), kind=kOutput, calls=%fused_computation.30 | convolution fusion | flops 1213071360 | bytes 3935232 | tf_op jit(solution)/shard_map/zk,yfxz->kfxy/dot_general | solution.py:82
  396.6 3.3 copy.31
  400.0 28.9 %all_to_all.89 = bf16[512,4,96,4]{2,1,3,0:T(4,128)(2,1)} all-to-all(bf16[512,4,96,4]{2,1,3,0:T(4,128)(2,1)S(1)} %copy.31), channel_id=1, replica_groups=mesh['kx'=8,'cz'=4] {'cz'}, dimensions={0} | all-to-all | bytes 3145728 | tf_op jit(solution)/shard_map/all_to_all | solution.py:85
  428.9 4.0 copy.32
  432.9 2.5 copy.33
  (7 shorter events, 0.0 us)
Async XLA Ops:
  4.5 24.3 %all-to-all-start = ((bf16[128,4,96,16]{0,2,1,3:T(8,128)(2,1)}), bf16[128,4,96,16]{0,2,1,3:T(8,128)(2,1)S(1)}, u32[]{:S(2)}, u32[]{:S(2)}) async-start(bf16[128,4,96,16]{0,2,1,3:T(8,128)(2,1)} %copy.19), calls=%async_computation | async-start | bytes 3145728 | tf_op jit(solution)/shard_map/all_to_all | solution.py:58
  28.8 23.6 %all-to-all-start.1 = ((bf16[128,4,96,16]{0,2,1,3:T(8,128)(2,1)}), bf16[128,4,96,16]{0,2,1,3:T(8,128)(2,1)S(1)}, u32[]{:S(2)}, u32[]{:S(2)}) async-start(bf16[128,4,96,16]{0,2,1,3:T(8,128)(2,1)} %copy.23), calls=%async_computation.1 | async-start | bytes 3145728 | tf_op jit(solution)/shard_map/all_to_all | solution.py:64
  53.6 2.0 copy-start.1
  55.6 9.7 %copy-start.2 = (bf16[512,4,96,4]{0,2,3,1:T(8,128)(2,1)S(1)}, bf16[512,4,96,4]{0,2,3,1:T(8,128)(2,1)}, u32[]{:S(2)}) copy-start(bf16[512,4,96,4]{0,2,3,1:T(8,128)(2,1)} %all_to_all.70) | copy-start | bytes 4718596
  251.1 12.7 %copy-start = (bf16[4,8,768,96]{2,3,1,0:T(8,128)(2,1)S(1)}, bf16[4,8,768,96]{2,3,1,0:T(8,128)(2,1)}, u32[]{:S(2)}) copy-start(bf16[4,8,768,96]{2,3,1,0:T(8,128)(2,1)} %all_to_all.74) | copy-start | bytes 14155780
where the time goes:
time: 444 us; the launch traced here: 436 us
  blocking collectives  247 us (56%)
  matrix products  79.8 us (18%)
  local copies, waits for them, and re-layouts  67.2 us (15%)
  waiting for transfers between devices  29.5 us (7%)
  starting transfers between devices  7.83 us (2%)
    all_to_all x1, blocking collectives, on_device(): lax.all_to_all(lifted, 'kx', split_axis=3, concat_axis=2, tiled=True)  145 us
    all_to_all x1, blocking collectives, on_device(): lax.all_to_all(turned, 'kx', split_axis=2, concat_axis=3, tiled=True)  73.6 us
    all_to_all x1, blocking collectives, on_device(): lax.all_to_all(spectral, 'cz', split_axis=0, concat_axis=3, tiled=True)  28.9 us
    dot_general x1, matrix products, on_device(): jnp.einsum('xm,yfmz->fyzx', hartley, piece[:, field_count:], preferred_el...  25.5 us
    all_to_all x2, local copies, waits for them, and re-layouts, on_device(): lax.all_to_all(lifted, 'kx', split_axis=3, concat_axis=2, tiled=True)  17.5 us
    all_to_all x1, waiting for transfers between devices, on_device(): lax.all_to_all(field_grid, 'cz', split_axis=3, concat_axis=0, tiled=True)  15.5 us
    all_to_all x1, waiting for transfers between devices, on_device(): lax.all_to_all(cotangent_grid, 'cz', split_axis=3, concat_axis=0, tiled=T...  14 us
    dot_general x1, matrix products, on_device(): jnp.einsum('xm,yfmz->fyzx', hartley, piece[:, :field_count], preferred_el...  12.7 us
  transfers between devices with their start and end apart: 2, of which 2 were waited for; matrix products, arithmetic and copies ran while one was open for 2% of the time, Pallas kernels for 0%

commit v1 on v0

v1 whole, which is shorter than its diff:
```python
import functools
import math

import jax
import jax.numpy as jnp
import numpy as np
from jax import lax
from jax.experimental import pallas as pl
from jax.experimental.pallas import tpu as pltpu
from jax.sharding import PartitionSpec as P

MZ = 768
Y = 16
MESH = pl.DeviceIdType.MESH


def cosine_table(rows, columns):
    position = (np.arange(columns)[None, :] * (2 * np.arange(rows)[:, None] + 1)) % (4 * rows)
    return np.cos(np.pi * position / (2 * rows)).astype(np.float32)


def hartley_table(points):
    index = np.arange(points)
    phases = 2.0 * np.pi * ((index[:, None] * index[None, :]) % points) / points
    return (np.cos(phases) + np.sin(phases)) / math.sqrt(points)


def matmul(a, b):
    return jnp.dot(a, b, preferred_element_type=jnp.float32)


def kernel(
    nkx, ncz, shares,
    field_src, adjoint_src, hartley, lift_fields, lift_adjoint, lower,
    out,
    held, mixed, halves, lowered, turned, result,
    in_send, in_recv, swap_send, swap_recv, back_send, back_recv, out_send, out_recv,
):
    rows_y, fields, local_m, local_k = field_src.shape
    per_share = ncz // shares
    points_x = hartley.shape[0]
    share_x = points_x // shares
    i, j = lax.axis_index("kx"), lax.axis_index("cz")
    linear = i * ncz + j
    my_y, my_share = linear // shares, lax.rem(linear, shares)
    to_share = j // per_share
    my_part = lax.rem(j, per_share)
    my_slot = i * per_share + my_part
    stays = to_share == my_share

    def device(target):
        return {"kx": target // ncz, "cz": lax.rem(target, ncz)}

    def held_at(a, kx, part):
        columns = pl.ds(pl.multiple_of(part * local_k, local_k), local_k) if per_share > 1 else slice(None)
        return held.at[pl.ds(a * fields, fields), pl.ds(pl.multiple_of(kx * local_m, local_m), local_m), columns]

    sources = (field_src, adjoint_src)

    def in_remote(a, y):
        return pltpu.make_async_remote_copy(
            src_ref=sources[a].at[y],
            dst_ref=held_at(a, i, my_part),
            send_sem=in_send.at[a, y],
            recv_sem=in_recv.at[a, my_slot],
            device_id=device(y * shares + to_share),
            device_id_type=MESH,
        )

    def in_local(a):
        return pltpu.make_async_copy(sources[a].at[my_y], held_at(a, i, my_part), in_recv.at[a, my_slot])

    for a in range(2):
        @pl.when(stays)
        def _():
            in_local(a).start()

        @pl.when(jnp.logical_not(stays))
        def _():
            in_remote(a, my_y).start()

        def send(step, carry):
            in_remote(a, lax.rem(my_y + step, rows_y)).start()
            return carry

        lax.fori_loop(1, rows_y, send, 0)

    def swap_rows(q):
        return pl.ds(pl.multiple_of(q * share_x, share_x), share_x)

    def swap(a, q):
        arrays = pl.ds(a * fields, fields)
        return pltpu.make_async_remote_copy(
            src_ref=mixed.at[arrays, swap_rows(q), :],
            dst_ref=halves.at[my_share, arrays],
            send_sem=swap_send.at[a, q],
            recv_sem=swap_recv.at[a, my_share],
            device_id=device(my_y * shares + q),
            device_id_type=MESH,
        )

    def swap_local(a):
        arrays = pl.ds(a * fields, fields)
        return pltpu.make_async_copy(
            mixed.at[arrays, swap_rows(my_share), :], halves.at[my_share, arrays], swap_recv.at[a, my_share]
        )

    for a in range(2):
        def arrive(slot, carry):
            pltpu.make_async_copy(
                sources[a].at[0], held_at(a, slot // per_share, lax.rem(slot, per_share)), in_recv.at[a, slot]
            ).wait()
            return carry

        lax.fori_loop(0, rows_y, arrive, 0)

        def mix(f, carry):
            mixed[a * fields + f] = matmul(hartley[...], held[a * fields + f]).astype(jnp.bfloat16)
            return carry

        lax.fori_loop(0, fields, mix, 0)
        swap_local(a).start()
        for step in range(1, shares):
            swap(a, lax.rem(my_share + step, shares)).start()

    for a in range(2):
        for q in range(shares):
            arrays = pl.ds(a * fields, fields)
            pltpu.make_async_copy(
                mixed.at[arrays, swap_rows(0), :], halves.at[q, arrays], swap_recv.at[a, q]
            ).wait()

    tile = 128 if share_x % 128 == 0 else share_x

    def products(step, carry):
        here = pl.ds(pl.multiple_of(step * tile, tile), tile)

        def lifted(a, f):
            table = (lift_fields, lift_adjoint)[a]
            total = matmul(halves[0, a * fields + f, here, :], table[0])
            for q in range(1, shares):
                total += matmul(halves[q, a * fields + f, here, :], table[q])
            return total

        def put(f, value):
            value = value.astype(jnp.bfloat16)
            for q in range(shares):
                lowered[q, f, here, :] = matmul(value, lower[q]).astype(jnp.bfloat16)

        vertical = lifted(0, 2)
        adjoint = lifted(1, 0)
        put(0, adjoint * vertical)
        total = adjoint * lifted(0, 0)
        adjoint = lifted(1, 1)
        put(1, adjoint * vertical)
        total += adjoint * lifted(0, 1)
        total += 2.0 * lifted(1, 2) * vertical
        adjoint = lifted(1, 3)
        put(3, adjoint * vertical)
        total += adjoint * lifted(0, 3)
        put(2, total)
        return carry

    lax.fori_loop(0, share_x // tile, products, 0)

    def back(q):
        return pltpu.make_async_remote_copy(
            src_ref=lowered.at[q],
            dst_ref=turned.at[:, swap_rows(my_share), :],
            send_sem=back_send.at[q],
            recv_sem=back_recv.at[my_share],
            device_id=device(my_y * shares + q),
            device_id_type=MESH,
        )

    back_local = pltpu.make_async_copy(
        lowered.at[my_share], turned.at[:, swap_rows(my_share), :], back_recv.at[my_share]
    )
    back_local.start()
    for step in range(1, shares):
        back(lax.rem(my_share + step, shares)).start()
    for q in range(shares):
        pltpu.make_async_copy(lowered.at[q], turned.at[:, swap_rows(q), :], back_recv.at[q]).wait()

    def result_at(f, slot):
        part = lax.rem(slot, per_share)
        columns = pl.ds(pl.multiple_of(part * local_k, local_k), local_k) if per_share > 1 else slice(None)
        rows = pl.ds(pl.multiple_of((slot // per_share) * local_m, local_m), local_m)
        return result.at[f, rows, columns]

    def owner(slot):
        return (slot // per_share) * ncz + my_share * per_share + lax.rem(slot, per_share)

    def out_remote(f, slot):
        return pltpu.make_async_remote_copy(
            src_ref=result_at(f, slot),
            dst_ref=out.at[my_y, f],
            send_sem=out_send.at[f, slot],
            recv_sem=out_recv.at[f, my_y],
            device_id=device(owner(slot)),
            device_id_type=MESH,
        )

    def out_local(f):
        return pltpu.make_async_copy(result_at(f, my_slot), out.at[my_y, f], out_recv.at[f, my_y])

    def finish(f, carry):
        result[f] = matmul(hartley[...], turned[f]).astype(jnp.bfloat16)

        @pl.when(stays)
        def _():
            out_local(f).start()

        @pl.when(jnp.logical_not(stays))
        def _():
            out_remote(f, my_slot).start()

        def send(step, inner):
            out_remote(f, lax.rem(my_slot + step, rows_y)).start()
            return inner

        lax.fori_loop(1, rows_y, send, 0)
        return carry

    lax.fori_loop(0, fields, finish, 0)

    for a in range(2):
        @pl.when(jnp.logical_not(stays))
        def _():
            in_remote(a, my_y).wait_send()

        def sent(step, carry):
            in_remote(a, lax.rem(my_y + step, rows_y)).wait_send()
            return carry

        lax.fori_loop(1, rows_y, sent, 0)
        for step in range(1, shares):
            swap(a, lax.rem(my_share + step, shares)).wait_send()
    for step in range(1, shares):
        back(lax.rem(my_share + step, shares)).wait_send()

    def close(f, carry):
        @pl.when(jnp.logical_not(stays))
        def _():
            out_remote(f, my_slot).wait_send()

        def sent(step, inner):
            out_remote(f, lax.rem(my_slot + step, rows_y)).wait_send()
            return inner

        lax.fori_loop(1, rows_y, sent, 0)

        def arrive(y, inner):
            pltpu.make_async_copy(result_at(0, 0), out.at[y, f], out_recv.at[f, y]).wait()
            return inner

        lax.fori_loop(0, rows_y, arrive, 0)
        return carry

    lax.fori_loop(0, fields, close, 0)


def on_device(nkx, ncz, field_modes, cotangent):
    local_k, fields, columns = field_modes.shape
    local_m = columns // Y
    modes_z, points_x = local_k * ncz, local_m * nkx
    shares = nkx * ncz // Y
    group_k = modes_z // shares
    share_x = points_x // shares
    bf16 = jnp.bfloat16

    def by_row(array):
        return array.reshape(local_k, fields, local_m, Y).transpose(3, 1, 2, 0)

    cosines = cosine_table(MZ, modes_z)
    synthesis = jnp.asarray((cosines * math.sqrt(2.0 / modes_z)).astype(bf16))
    projection = jnp.asarray((cosines * math.sqrt(2.0 / MZ)).astype(bf16))
    hartley = jnp.asarray(hartley_table(points_x).astype(np.float32).astype(bf16))
    lift_fields = synthesis.T.reshape(shares, group_k, MZ)
    lift_adjoint = projection.T.reshape(shares, group_k, MZ)
    lower = synthesis.reshape(MZ, shares, group_k).transpose(1, 0, 2)

    vmem = pl.BlockSpec(memory_space=pltpu.VMEM)
    dma = pltpu.SemaphoreType.DMA
    out = pl.pallas_call(
        functools.partial(kernel, nkx, ncz, shares),
        out_shape=jax.ShapeDtypeStruct((Y, fields, local_m, local_k), bf16),
        in_specs=[vmem] * 6,
        out_specs=pl.BlockSpec(memory_space=pl.ANY),
        scratch_shapes=[
            pltpu.VMEM((2 * fields, points_x, group_k), bf16),
            pltpu.VMEM((2 * fields, points_x, group_k), bf16),
            pltpu.VMEM((shares, 2 * fields, share_x, group_k), bf16),
            pltpu.VMEM((shares, fields, share_x, group_k), bf16),
            pltpu.VMEM((fields, points_x, group_k), bf16),
            pltpu.VMEM((fields, points_x, group_k), bf16),
            dma((2, Y)), dma((2, Y)), dma((2, shares)), dma((2, shares)),
            dma((shares,)), dma((shares,)), dma((fields, Y)), dma((fields, Y)),
        ],
        compiler_params=pltpu.CompilerParams(has_side_effects=True, vmem_limit_bytes=48 * 2**20),
    )(by_row(field_modes), by_row(cotangent), hartley, lift_fields, lift_adjoint, lower)
    return out.transpose(3, 1, 2, 0).reshape(local_k, fields, columns)


def solution(mesh):
    return jax.shard_map(
        functools.partial(on_device, mesh.shape["kx"], mesh.shape["cz"]),
        mesh=mesh,
        in_specs=(P("cz", None, "kx"), P("cz", None, "kx")),
        out_specs=P("cz", None, "kx"),
        check_vma=False,
    )
```

time: 444 us -> 139 us (0.31)
  the two profiles are of different devices: /device:TPU:0 before, /device:TPU:27 now
where the time goes in v1:
time: 139 us
  Pallas kernels  127 us (91%)
  local copies, waits for them, and re-layouts  12 us (9%)
    pallas_call x1, Pallas kernels, on_device(): pl.pallas_call(functools.partial(kernel, nkx, ncz, shares), out_shape=jax...  127 us
    unnamed x10, local copies, waits for them, and re-layouts  5.94 us

profile of v1, /device:TPU:27, one launch (start us, length us, event | category | flops | bytes accessed | tf_op | source)
XLA Modules:
  0.0 138.7 jit_solution(4253028606910148118)
XLA Ops:
  0.0 3.0 %copy.6 = bf16[128,4,1536]{0,2,1:T(8,128)(2,1)S(1)} copy(bf16[128,4,1536]{2,1,0:T(4,128)(2,1)} %param.5) | data formatting | bytes 3145728 | tf_op args[0]
  3.0 3.0 %copy.8 = bf16[128,4,1536]{0,2,1:T(8,128)(2,1)S(1)} copy(bf16[128,4,1536]{2,1,0:T(4,128)(2,1)} %param.6) | data formatting | bytes 3145728 | tf_op args[1]
  5.9 0.0 copy-start
  5.9 0.0 copy-start.1
  6.0 0.0 copy-start.2
  6.0 0.0 copy-start.3
  6.0 2.6 %copy_bitcast_fusion = (bf16[16,4,96,128]{3,2,1,0:T(8,128)(2,1)}, bf16[16,4,96,128]{3,2,1,0:T(8,128)(2,1)}) fusion(bf16[128,4,96,16]{0,3,2,1:T(8,128)(2,1)S(1)} %bitcast.11, bf16[128,4,96,16]{0,3,2,1:T(8,128)(2,1)S(1)} %bitcast.10), kind=kLoop, calls=%fused_computation | loop fusion | bytes 6291456 | tf_op jit(solution)/shard_map/transpose | solution.py:273
  8.6 0.0 copy-done
  8.6 0.0 copy-done.1
  8.6 0.0 copy-done.2
  8.6 0.0 copy-done.3
  8.6 126.6 %shard_map.55 = bf16[16,4,96,128]{3,2,1,0:T(8,128)(2,1)S(1)} custom-call(bf16[16,4,96,128]{3,2,1,0:T(8,128)(2,1)} %get-tuple-element.6.field_src, bf16[16,4,96,128]{3,2,1,0:T(8,128)(2,1)} %get-tuple-element.5.adjoint_src, bf16[768,768]{1,0:T(8,128)(2,1)S(1)} %copy-done, bf16[2,256,768]{2,1,0:T(8,128)(2,1)S(1)} %copy-done.3, ...), custom_call_target="tpu_custom_call" | custom-call | tf_op jit(solution)/shard_map/pallas_call | solution.py:285
  135.2 1.0 copy.10
  136.2 2.5 %copy.11 = bf16[128,4,1536]{2,1,0:T(4,128)(2,1)} copy(bf16[128,4,1536]{0,2,1:T(8,128)(2,1)S(1)} %bitcast.9) | data formatting | bytes 3145728 | tf_op jit(solution)/shard_map/reshape | solution.py:302
Async XLA Ops:
  5.9 2.7 %copy-start = (bf16[768,768]{1,0:T(8,128)(2,1)S(1)}, bf16[768,768]{1,0:T(8,128)(2,1)}, u32[]{:S(2)}) copy-start(bf16[768,768]{1,0:T(8,128)(2,1)} %constant.8.clone.hartley) | copy-start | bytes 3538948
  5.9 2.7 %copy-start.1 = (bf16[2,768,256]{2,1,0:T(8,128)(2,1)S(1)}, bf16[2,768,256]{2,1,0:T(8,128)(2,1)}, u32[]{:S(2)}) copy-start(bf16[2,768,256]{2,1,0:T(8,128)(2,1)} %constant.14.lower) | copy-start | bytes 2359300
  6.0 2.7 %copy-start.2 = (bf16[2,256,768]{2,1,0:T(8,128)(2,1)S(1)}, bf16[2,256,768]{2,1,0:T(8,128)(2,1)}, u32[]{:S(2)}) copy-start(bf16[2,256,768]{2,1,0:T(8,128)(2,1)} %constant.12.lift_adjoint) | copy-start | bytes 2359300
  6.0 2.6 %copy-start.3 = (bf16[2,256,768]{2,1,0:T(8,128)(2,1)S(1)}, bf16[2,256,768]{2,1,0:T(8,128)(2,1)}, u32[]{:S(2)}) copy-start(bf16[2,256,768]{2,1,0:T(8,128)(2,1)} %constant.10.lift_fields) | copy-start | bytes 2359300

commit v2 on v1

v2 whole, which is shorter than its diff:
```python
import functools
import math

import jax
import jax.numpy as jnp
import numpy as np
from jax import lax
from jax.experimental import pallas as pl
from jax.experimental.pallas import tpu as pltpu
from jax.sharding import PartitionSpec as P

MZ = 768
Y = 16
MESH = pl.DeviceIdType.MESH


def cosine_table(rows, columns):
    position = (np.arange(columns)[None, :] * (2 * np.arange(rows)[:, None] + 1)) % (4 * rows)
    return np.cos(np.pi * position / (2 * rows)).astype(np.float32)


def hartley_table(points):
    index = np.arange(points)
    phases = 2.0 * np.pi * ((index[:, None] * index[None, :]) % points) / points
    return (np.cos(phases) + np.sin(phases)) / math.sqrt(points)


def matmul(a, b):
    return jnp.dot(a, b, preferred_element_type=jnp.float32)


def kernel(
    nkx, ncz, shares,
    field_src, adjoint_src, hartley, lift_fields, lift_adjoint, lower,
    out,
    held, mixed, halves, points, total, flux, lowered, turned, result,
    in_send, in_recv, swap_send, swap_recv, back_send, back_recv, out_send, out_recv,
):
    rows_y, fields, local_m, local_k = field_src.shape
    per_share = ncz // shares
    points_x = hartley.shape[0]
    points_z = lift_fields.shape[2]
    share_x = points_x // shares
    i, j = lax.axis_index("kx"), lax.axis_index("cz")
    linear = i * ncz + j
    my_y, my_share = linear // shares, lax.rem(linear, shares)
    to_share = j // per_share
    my_part = lax.rem(j, per_share)
    my_slot = i * per_share + my_part
    stays = to_share == my_share
    far = rows_y // 2
    order = ((0, 2), (1, 0), (1, 1), (1, 3), (0, 0), (0, 1), (0, 3), (1, 2))
    sources = (field_src, adjoint_src)
    tables = (lift_fields, lift_adjoint)

    def device(target):
        return {"kx": target // ncz, "cz": lax.rem(target, ncz)}

    def block(ref, slot):
        part = lax.rem(slot, per_share)
        rows = pl.ds(pl.multiple_of((slot // per_share) * local_m, local_m), local_m)
        columns = pl.ds(pl.multiple_of(part * local_k, local_k), local_k) if per_share > 1 else slice(None)
        return ref.at[rows, columns]

    def other(mine, step):
        half = jnp.where(step < far, 1 - mine // far, mine // far)
        return half * far + lax.rem(mine + 1 + step, far)

    def wait(ref, sem):
        pltpu.make_async_copy(ref, ref, sem).wait()

    def in_remote(h, y):
        a, f = order[h]
        return pltpu.make_async_remote_copy(
            src_ref=sources[a].at[y, f],
            dst_ref=block(held.at[h], my_slot),
            send_sem=in_send.at[a],
            recv_sem=in_recv.at[h],
            device_id=device(y * shares + to_share),
            device_id_type=MESH,
        )

    for h, (a, f) in enumerate(order):
        def send(step, carry):
            in_remote(h, other(my_y, step)).start()
            return carry

        lax.fori_loop(0, rows_y - 1, send, 0)

        @pl.when(stays)
        def _():
            pltpu.make_async_copy(sources[a].at[my_y, f], block(held.at[h], my_slot), in_recv.at[h]).start()

        @pl.when(jnp.logical_not(stays))
        def _():
            in_remote(h, my_y).start()

    def share_rows(q):
        return pl.ds(pl.multiple_of(q * share_x, share_x), share_x)

    def mix(h):
        wait(held.at[h], in_recv.at[h])
        mixed[h] = matmul(hartley[...], held[h]).astype(jnp.bfloat16)
        for step in range(1, shares):
            q = lax.rem(my_share + step, shares)
            pltpu.make_async_remote_copy(
                src_ref=mixed.at[h, share_rows(q), :],
                dst_ref=halves.at[h, my_share],
                send_sem=swap_send,
                recv_sem=swap_recv.at[h],
                device_id=device(my_y * shares + q),
                device_id_type=MESH,
            ).start()
        pltpu.make_async_copy(
            mixed.at[h, share_rows(my_share), :], halves.at[h, my_share], swap_recv.at[h]
        ).start()

    block_z = 256 if points_z % 256 == 0 else points_z

    def lift(h, use):
        wait(halves.at[h], swap_recv.at[h])
        table = tables[order[h][0]]

        def one(step, carry):
            here = pl.ds(pl.multiple_of(step * block_z, block_z), block_z)
            value = matmul(halves[h, 0], table[0, :, here])
            for q in range(1, shares):
                value += matmul(halves[h, q], table[q, :, here])
            use(here, value)
            return carry

        lax.fori_loop(0, points_z // block_z, one, 0)

    def leave(f):
        for q in range(shares):
            lowered[f, q] = matmul(flux[...], lower[q]).astype(jnp.bfloat16)
        for step in range(1, shares):
            q = lax.rem(my_share + step, shares)
            pltpu.make_async_remote_copy(
                src_ref=lowered.at[f, q],
                dst_ref=turned.at[f, share_rows(my_share), :],
                send_sem=back_send,
                recv_sem=back_recv.at[f],
                device_id=device(my_y * shares + q),
                device_id_type=MESH,
            ).start()
        pltpu.make_async_copy(
            lowered.at[f, my_share], turned.at[f, share_rows(my_share), :], back_recv.at[f]
        ).start()

    def out_remote(f, slot):
        target = (slot // per_share) * ncz + my_share * per_share + lax.rem(slot, per_share)
        return pltpu.make_async_remote_copy(
            src_ref=block(result.at[f], slot),
            dst_ref=out.at[my_y, f],
            send_sem=out_send,
            recv_sem=out_recv.at[f],
            device_id=device(target),
            device_id_type=MESH,
        )

    def finish(f):
        wait(turned.at[f], back_recv.at[f])
        result[f] = matmul(hartley[...], turned[f]).astype(jnp.bfloat16)

        def send(step, carry):
            out_remote(f, other(my_slot, step)).start()
            return carry

        lax.fori_loop(0, rows_y - 1, send, 0)

        @pl.when(stays)
        def _():
            pltpu.make_async_copy(block(result.at[f], my_slot), out.at[my_y, f], out_recv.at[f]).start()

        @pl.when(jnp.logical_not(stays))
        def _():
            out_remote(f, my_slot).start()

    def keep(h):
        def use(here, value):
            points[h, :, here] = value
        return use

    def keep_and_flux(h):
        def use(here, value):
            points[h, :, here] = value
            flux[:, here] = (value * points[0, :, here]).astype(jnp.bfloat16)
        return use

    def first(here, value):
        total[:, here] = points[1, :, here] * value

    def add(h):
        def use(here, value):
            total[:, here] += points[h, :, here] * value
        return use

    def last(here, value):
        flux[:, here] = (total[:, here] + 2.0 * value * points[0, :, here]).astype(jnp.bfloat16)

    mix(0)
    mix(1)
    lift(0, keep(0))
    lift(1, keep_and_flux(1))
    leave(0)
    mix(2)
    finish(0)
    lift(2, keep_and_flux(2))
    leave(1)
    mix(3)
    finish(1)
    lift(3, keep_and_flux(3))
    leave(3)
    mix(4)
    finish(3)
    lift(4, first)
    mix(5)
    lift(5, add(2))
    mix(6)
    lift(6, add(3))
    mix(7)
    lift(7, last)
    leave(2)
    finish(2)

    for a in range(2):
        @pl.when(stays)
        def _():
            wait(sources[a].at[pl.ds(0, rows_y - 1)], in_send.at[a])

        @pl.when(jnp.logical_not(stays))
        def _():
            wait(sources[a], in_send.at[a])

    if shares > 1:
        wait(mixed.at[:, pl.ds(0, share_x * (shares - 1)), :], swap_send)
        wait(lowered.at[:, pl.ds(0, shares - 1)], back_send)

    @pl.when(stays)
    def _():
        wait(out.at[pl.ds(0, rows_y - 1)], out_send)

    @pl.when(jnp.logical_not(stays))
    def _():
        wait(out, out_send)

    for f in range(fields):
        wait(out.at[:, f], out_recv.at[f])


def on_device(nkx, ncz, field_modes, cotangent):
    local_k, fields, columns = field_modes.shape
    local_m = columns // Y
    modes_z, points_x = local_k * ncz, local_m * nkx
    shares = nkx * ncz // Y
    group_k = modes_z // shares
    share_x = points_x // shares
    bf16 = jnp.bfloat16

    def by_row(array):
        return array.reshape(local_k, fields, local_m, Y).transpose(3, 1, 2, 0)

    cosines = cosine_table(MZ, modes_z)
    synthesis = jnp.asarray((cosines * math.sqrt(2.0 / modes_z)).astype(bf16))
    projection = jnp.asarray((cosines * math.sqrt(2.0 / MZ)).astype(bf16))
    hartley = jnp.asarray(hartley_table(points_x).astype(np.float32).astype(bf16))
    lift_fields = synthesis.T.reshape(shares, group_k, MZ)
    lift_adjoint = projection.T.reshape(shares, group_k, MZ)
    lower = synthesis.reshape(MZ, shares, group_k).transpose(1, 0, 2)

    vmem = pl.BlockSpec(memory_space=pltpu.VMEM)
    dma = pltpu.SemaphoreType.DMA
    out = pl.pallas_call(
        functools.partial(kernel, nkx, ncz, shares),
        out_shape=jax.ShapeDtypeStruct((Y, fields, local_m, local_k), bf16),
        in_specs=[vmem] * 6,
        out_specs=pl.BlockSpec(memory_space=pl.ANY),
        scratch_shapes=[
            pltpu.VMEM((2 * fields, points_x, group_k), bf16),
            pltpu.VMEM((2 * fields, points_x, group_k), bf16),
            pltpu.VMEM((2 * fields, shares, share_x, group_k), bf16),
            pltpu.VMEM((fields, share_x, MZ), jnp.float32),
            pltpu.VMEM((share_x, MZ), jnp.float32),
            pltpu.VMEM((share_x, MZ), bf16),
            pltpu.VMEM((fields, shares, share_x, group_k), bf16),
            pltpu.VMEM((fields, points_x, group_k), bf16),
            pltpu.VMEM((fields, points_x, group_k), bf16),
            dma((2,)), dma((2 * fields,)), dma, dma((2 * fields,)),
            dma, dma((fields,)), dma, dma((fields,)),
        ],
        compiler_params=pltpu.CompilerParams(has_side_effects=True, vmem_limit_bytes=48 * 2**20),
    )(by_row(field_modes), by_row(cotangent), hartley, lift_fields, lift_adjoint, lower)
    return out.transpose(3, 1, 2, 0).reshape(local_k, fields, columns)


def solution(mesh):
    return jax.shard_map(
        functools.partial(on_device, mesh.shape["kx"], mesh.shape["cz"]),
        mesh=mesh,
        in_specs=(P("cz", None, "kx"), P("cz", None, "kx")),
        out_specs=P("cz", None, "kx"),
        check_vma=False,
    )
```

time: 139 us -> 128 us (0.921)
  the two profiles are of different devices: /device:TPU:27 before, /device:TPU:0 now
where the time goes in v2:
time: 128 us
  Pallas kernels  116 us (91%)
  local copies, waits for them, and re-layouts  12 us (9%)
    pallas_call x1, Pallas kernels, on_device(): pl.pallas_call(functools.partial(kernel, nkx, ncz, shares), out_shape=jax...  116 us
    unnamed x10, local copies, waits for them, and re-layouts  5.94 us
    transpose x1, local copies, waits for them, and re-layouts, by_row(): return array.reshape(local_k, fields, local_m, Y).transpose(3, 1, 2, 0)  2.62 us

profile of v2, /device:TPU:0, one launch (start us, length us, event | category | flops | bytes accessed | tf_op | source)
XLA Modules:
  0.0 127.6 jit_solution(7993772287174143364)
XLA Ops:
  0.0 3.0 %copy.6 = bf16[128,4,1536]{0,2,1:T(8,128)(2,1)S(1)} copy(bf16[128,4,1536]{2,1,0:T(4,128)(2,1)} %param.5) | data formatting | bytes 3145728 | tf_op args[0]
  3.0 3.0 %copy.8 = bf16[128,4,1536]{0,2,1:T(8,128)(2,1)S(1)} copy(bf16[128,4,1536]{2,1,0:T(4,128)(2,1)} %param.6) | data formatting | bytes 3145728 | tf_op args[1]
  5.9 0.0 copy-start
  5.9 0.0 copy-start.1
  6.0 0.0 copy-start.2
  6.0 0.0 copy-start.3
  6.0 2.6 %copy_bitcast_fusion = (bf16[16,4,96,128]{3,2,1,0:T(8,128)(2,1)}, bf16[16,4,96,128]{3,2,1,0:T(8,128)(2,1)}) fusion(bf16[128,4,96,16]{0,3,2,1:T(8,128)(2,1)S(1)} %bitcast.11, bf16[128,4,96,16]{0,3,2,1:T(8,128)(2,1)S(1)} %bitcast.10), kind=kLoop, calls=%fused_computation | loop fusion | bytes 6291456 | tf_op jit(solution)/shard_map/transpose | solution.py:262
  8.6 0.0 copy-done
  8.6 0.0 copy-done.1
  8.6 0.0 copy-done.2
  8.6 0.0 copy-done.3
  8.6 115.5 %shard_map.55 = bf16[16,4,96,128]{3,2,1,0:T(8,128)(2,1)S(1)} custom-call(bf16[16,4,96,128]{3,2,1,0:T(8,128)(2,1)} %get-tuple-element.6.field_src, bf16[16,4,96,128]{3,2,1,0:T(8,128)(2,1)} %get-tuple-element.5.adjoint_src, bf16[768,768]{1,0:T(8,128)(2,1)S(1)} %copy-done, bf16[2,256,768]{2,1,0:T(8,128)(2,1)S(1)} %copy-done.3, ...), custom_call_target="tpu_custom_call" | custom-call | tf_op jit(solution)/shard_map/pallas_call | solution.py:274
  124.2 1.0 copy.10
  125.2 2.5 %copy.11 = bf16[128,4,1536]{2,1,0:T(4,128)(2,1)} copy(bf16[128,4,1536]{0,2,1:T(8,128)(2,1)S(1)} %bitcast.9) | data formatting | bytes 3145728 | tf_op jit(solution)/shard_map/reshape | solution.py:294
Async XLA Ops:
  5.9 2.7 %copy-start = (bf16[768,768]{1,0:T(8,128)(2,1)S(1)}, bf16[768,768]{1,0:T(8,128)(2,1)}, u32[]{:S(2)}) copy-start(bf16[768,768]{1,0:T(8,128)(2,1)} %constant.8.clone.hartley) | copy-start | bytes 3538948
  5.9 2.7 %copy-start.1 = (bf16[2,768,256]{2,1,0:T(8,128)(2,1)S(1)}, bf16[2,768,256]{2,1,0:T(8,128)(2,1)}, u32[]{:S(2)}) copy-start(bf16[2,768,256]{2,1,0:T(8,128)(2,1)} %constant.14.lower) | copy-start | bytes 2359300
  6.0 2.7 %copy-start.2 = (bf16[2,256,768]{2,1,0:T(8,128)(2,1)S(1)}, bf16[2,256,768]{2,1,0:T(8,128)(2,1)}, u32[]{:S(2)}) copy-start(bf16[2,256,768]{2,1,0:T(8,128)(2,1)} %constant.12.lift_adjoint) | copy-start | bytes 2359300
  6.0 2.6 %copy-start.3 = (bf16[2,256,768]{2,1,0:T(8,128)(2,1)S(1)}, bf16[2,256,768]{2,1,0:T(8,128)(2,1)}, u32[]{:S(2)}) copy-start(bf16[2,256,768]{2,1,0:T(8,128)(2,1)} %constant.10.lift_fields) | copy-start | bytes 2359300

commit v3 on v2

--- a/solution.py
+++ b/solution.py
@@ -31,12 +31,14 @@
 
 def kernel(
     nkx, ncz, shares,
-    field_src, adjoint_src, hartley, lift_fields, lift_adjoint, lower,
+    field_modes, cotangent, hartley, lift_fields, lift_adjoint, lower,
     out,
-    held, mixed, halves, points, total, flux, lowered, turned, result,
+    wide, rows, held, mixed, halves, points, total, flux, lowered, turned, result,
     in_send, in_recv, swap_send, swap_recv, back_send, back_recv, out_send, out_recv,
 ):
-    rows_y, fields, local_m, local_k = field_src.shape
+    local_k, fields, columns = field_modes.shape
+    rows_y = rows.shape[1]
+    local_m = columns // rows_y
     per_share = ncz // shares
     points_x = hartley.shape[0]
     points_z = lift_fields.shape[2]
@@ -50,7 +52,7 @@
     stays = to_share == my_share
     far = rows_y // 2
     order = ((0, 2), (1, 0), (1, 1), (1, 3), (0, 0), (0, 1), (0, 3), (1, 2))
-    sources = (field_src, adjoint_src)
+    sources = (field_modes, cotangent)
     tables = (lift_fields, lift_adjoint)
 
     def device(target):
@@ -70,17 +72,27 @@
         pltpu.make_async_copy(ref, ref, sem).wait()
 
     def in_remote(h, y):
-        a, f = order[h]
         return pltpu.make_async_remote_copy(
-            src_ref=sources[a].at[y, f],
+            src_ref=rows.at[h, y],
             dst_ref=block(held.at[h], my_slot),
-            send_sem=in_send.at[a],
+            send_sem=in_send,
             recv_sem=in_recv.at[h],
             device_id=device(y * shares + to_share),
             device_id_type=MESH,
         )
 
+    chunk = 128 if columns % 128 == 0 else columns
+
     for h, (a, f) in enumerate(order):
+        def turn(step, carry):
+            here = pl.ds(pl.multiple_of(step * chunk, chunk), chunk)
+            wide[here, :] = sources[a][:, f, here].astype(jnp.float32).T
+            return carry
+
+        lax.fori_loop(0, columns // chunk, turn, 0)
+        for y in range(rows_y):
+            rows[h, y] = wide[pl.ds(y, local_m, stride=rows_y), :].astype(jnp.bfloat16)
+
         def send(step, carry):
             in_remote(h, other(my_y, step)).start()
             return carry
@@ -89,7 +101,7 @@
 
         @pl.when(stays)
         def _():
-            pltpu.make_async_copy(sources[a].at[my_y, f], block(held.at[h], my_slot), in_recv.at[h]).start()
+            pltpu.make_async_copy(rows.at[h, my_y], block(held.at[h], my_slot), in_recv.at[h]).start()
 
         @pl.when(jnp.logical_not(stays))
         def _():
@@ -224,14 +236,13 @@
     leave(2)
     finish(2)
 
-    for a in range(2):
-        @pl.when(stays)
-        def _():
-            wait(sources[a].at[pl.ds(0, rows_y - 1)], in_send.at[a])
-
-        @pl.when(jnp.logical_not(stays))
-        def _():
-            wait(sources[a], in_send.at[a])
+    @pl.when(stays)
+    def _():
+        wait(rows.at[:, pl.ds(0, rows_y - 1)], in_send)
+
+    @pl.when(jnp.logical_not(stays))
+    def _():
+        wait(rows, in_send)
 
     if shares > 1:
         wait(mixed.at[:, pl.ds(0, share_x * (shares - 1)), :], swap_send)
@@ -258,9 +269,6 @@
     share_x = points_x // shares
     bf16 = jnp.bfloat16
 
-    def by_row(array):
-        return array.reshape(local_k, fields, local_m, Y).transpose(3, 1, 2, 0)
-
     cosines = cosine_table(MZ, modes_z)
     synthesis = jnp.asarray((cosines * math.sqrt(2.0 / modes_z)).astype(bf16))
     projection = jnp.asarray((cosines * math.sqrt(2.0 / MZ)).astype(bf16))
@@ -277,6 +285,8 @@
         in_specs=[vmem] * 6,
         out_specs=pl.BlockSpec(memory_space=pl.ANY),
         scratch_shapes=[
+            pltpu.VMEM((columns, local_k), jnp.float32),
+            pltpu.VMEM((2 * fields, Y, local_m, local_k), bf16),
             pltpu.VMEM((2 * fields, points_x, group_k), bf16),
             pltpu.VMEM((2 * fields, points_x, group_k), bf16),
             pltpu.VMEM((2 * fields, shares, share_x, group_k), bf16),
@@ -286,11 +296,11 @@
             pltpu.VMEM((fields, shares, share_x, group_k), bf16),
             pltpu.VMEM((fields, points_x, group_k), bf16),
             pltpu.VMEM((fields, points_x, group_k), bf16),
-            dma((2,)), dma((2 * fields,)), dma, dma((2 * fields,)),
+            dma, dma((2 * fields,)), dma, dma((2 * fields,)),
             dma, dma((fields,)), dma, dma((fields,)),
         ],
         compiler_params=pltpu.CompilerParams(has_side_effects=True, vmem_limit_bytes=48 * 2**20),
-    )(by_row(field_modes), by_row(cotangent), hartley, lift_fields, lift_adjoint, lower)
+    )(field_modes, cotangent, hartley, lift_fields, lift_adjoint, lower)
     return out.transpose(3, 1, 2, 0).reshape(local_k, fields, columns)
 
 

time: 128 us -> 126 us (0.984)
  local copies, waits for them, and re-layouts: 12 us -> 8.15 us
    transpose x1 -> x0, local copies, waits for them, and re-layouts: 2.62 us -> none  [by_row(): return array.reshape(local_k, fields, local_m, Y).transpose(3, 1, 2, 0)]
    pallas_call x1, Pallas kernels: 116 us -> 117 us  [on_device(): pl.pallas_call(functools.partial(kernel, nkx, ncz, shares), out_shape=jax...]
    unnamed x10 -> x8, local copies, waits for them, and re-layouts: 5.94 us -> 4.67 us
where the time goes in v3:
time: 126 us; the launch traced here: 125 us
  Pallas kernels  117 us (93%)
  local copies, waits for them, and re-layouts  8.15 us (6%)
    pallas_call x1, Pallas kernels, on_device(): pl.pallas_call(functools.partial(kernel, nkx, ncz, shares), out_shape=jax...  117 us
    unnamed x8, local copies, waits for them, and re-layouts  4.67 us

profile of v3, /device:TPU:0, one launch (start us, length us, event | category | flops | bytes accessed | tf_op | source)
XLA Modules:
  0.0 125.5 jit_solution(5652660465960490361)
XLA Ops:
  0.0 0.0 copy-start
  0.0 1.3 %copy-done = bf16[768,768]{1,0:T(8,128)(2,1)S(1)} copy-done((bf16[768,768]{1,0:T(8,128)(2,1)S(1)}, bf16[768,768]{1,0:T(8,128)(2,1)}, u32[]{:S(2)}) %copy-start) | copy-done | bytes 1179672
  1.3 0.0 copy-start.1
  1.3 1.1 copy-done.1
  2.4 0.0 copy-start.2
  2.4 1.1 copy-done.2
  3.5 0.0 copy-start.3
  3.5 1.1 copy-done.3
  4.7 117.3 %shard_map.55 = bf16[16,4,96,128]{3,2,1,0:T(8,128)(2,1)S(1)} custom-call(bf16[128,4,1536]{2,1,0:T(4,128)(2,1)} %field_modes.1, bf16[128,4,1536]{2,1,0:T(4,128)(2,1)} %cotangent.1, bf16[768,768]{1,0:T(8,128)(2,1)S(1)} %copy-done, bf16[2,256,768]{2,1,0:T(8,128)(2,1)S(1)} %copy-done.3, bf16[2,256,768]{2,1,0:T(8,128)(2,1)S(1)} %copy-done.2, ...), custom_call_target="tpu_custom_call" | custom-call | tf_op jit(solution)/shard_map/pallas_call | solution.py:282
  122.0 1.0 copy.6
  123.0 2.5 %copy.7 = bf16[128,4,1536]{2,1,0:T(4,128)(2,1)} copy(bf16[128,4,1536]{0,2,1:T(8,128)(2,1)S(1)} %bitcast.3) | data formatting | bytes 3145728 | tf_op jit(solution)/shard_map/reshape | solution.py:304
Async XLA Ops:
  0.0 1.3 %copy-start = (bf16[768,768]{1,0:T(8,128)(2,1)S(1)}, bf16[768,768]{1,0:T(8,128)(2,1)}, u32[]{:S(2)}) copy-start(bf16[768,768]{1,0:T(8,128)(2,1)} %constant.8.clone.hartley) | copy-start | bytes 3538948
  1.3 1.1 copy-start.1
  2.4 1.1 copy-start.2
  3.5 1.1 copy-start.3

commit v4 on v3

--- a/solution.py
+++ b/solution.py
@@ -31,8 +31,9 @@
 
 def kernel(
     nkx, ncz, shares,
-    field_modes, cotangent, hartley, lift_fields, lift_adjoint, lower,
+    field_modes, cotangent, hartley_in, lift_fields_in, lift_adjoint_in, lower_in,
     out,
+    raw, hartley, lift_fields, lift_adjoint, lower, raw_sem, table_sem,
     wide, rows, held, mixed, halves, points, total, flux, lowered, turned, result,
     in_send, in_recv, swap_send, swap_recv, back_send, back_recv, out_send, out_recv,
 ):
@@ -52,7 +53,22 @@
     stays = to_share == my_share
     far = rows_y // 2
     order = ((0, 2), (1, 0), (1, 1), (1, 3), (0, 0), (0, 1), (0, 3), (1, 2))
-    sources = (field_modes, cotangent)
+    raw_copies = [
+        pltpu.make_async_copy(array, raw.at[a], raw_sem.at[a]) for a, array in enumerate((field_modes, cotangent))
+    ]
+    table_copies = [
+        pltpu.make_async_copy(source, target, table_sem.at[n])
+        for n, (source, target) in enumerate(
+            (
+                (hartley_in, hartley),
+                (lift_fields_in, lift_fields),
+                (lift_adjoint_in, lift_adjoint),
+                (lower_in, lower),
+            )
+        )
+    ]
+    for copy in raw_copies + table_copies:
+        copy.start()
     tables = (lift_fields, lift_adjoint)
 
     def device(target):
@@ -84,9 +100,12 @@
     chunk = 128 if columns % 128 == 0 else columns
 
     for h, (a, f) in enumerate(order):
+        if h < 2:
+            raw_copies[h].wait()
+
         def turn(step, carry):
             here = pl.ds(pl.multiple_of(step * chunk, chunk), chunk)
-            wide[here, :] = sources[a][:, f, here].astype(jnp.float32).T
+            wide[here, :] = raw[a, :, f, here].astype(jnp.float32).T
             return carry
 
         lax.fori_loop(0, columns // chunk, turn, 0)
@@ -211,6 +230,8 @@
     def last(here, value):
         flux[:, here] = (total[:, here] + 2.0 * value * points[0, :, here]).astype(jnp.bfloat16)
 
+    for copy in table_copies:
+        copy.wait()
     mix(0)
     mix(1)
     lift(0, keep(0))
@@ -277,14 +298,20 @@
     lift_adjoint = projection.T.reshape(shares, group_k, MZ)
     lower = synthesis.reshape(MZ, shares, group_k).transpose(1, 0, 2)
 
-    vmem = pl.BlockSpec(memory_space=pltpu.VMEM)
+    hbm = pl.BlockSpec(memory_space=pltpu.HBM)
     dma = pltpu.SemaphoreType.DMA
     out = pl.pallas_call(
         functools.partial(kernel, nkx, ncz, shares),
         out_shape=jax.ShapeDtypeStruct((Y, fields, local_m, local_k), bf16),
-        in_specs=[vmem] * 6,
+        in_specs=[hbm] * 6,
         out_specs=pl.BlockSpec(memory_space=pl.ANY),
         scratch_shapes=[
+            pltpu.VMEM((2, local_k, fields, columns), bf16),
+            pltpu.VMEM(hartley.shape, bf16),
+            pltpu.VMEM(lift_fields.shape, bf16),
+            pltpu.VMEM(lift_adjoint.shape, bf16),
+            pltpu.VMEM(lower.shape, bf16),
+            dma((2,)), dma((4,)),
             pltpu.VMEM((columns, local_k), jnp.float32),
             pltpu.VMEM((2 * fields, Y, local_m, local_k), bf16),
             pltpu.VMEM((2 * fields, points_x, group_k), bf16),

time: 126 us -> 125 us (level)
  no operation moved by 1% of the time
where the time goes in v4:
time: 125 us
  Pallas kernels  117 us (94%)
  local copies, waits for them, and re-layouts  8.15 us (7%)
    pallas_call x1, Pallas kernels, on_device(): pl.pallas_call(functools.partial(kernel, nkx, ncz, shares), out_shape=jax...  117 us
    unnamed x8, local copies, waits for them, and re-layouts  4.67 us

profile of v4, /device:TPU:0, one launch (start us, length us, event | category | flops | bytes accessed | tf_op | source)
XLA Modules:
  0.0 125.0 jit_solution(18315026439999730684)
XLA Ops:
  0.0 0.0 copy-start
  0.0 1.3 %copy-done = bf16[768,768]{1,0:T(8,128)(2,1)S(1)} copy-done((bf16[768,768]{1,0:T(8,128)(2,1)S(1)}, bf16[768,768]{1,0:T(8,128)(2,1)}, u32[]{:S(2)}) %copy-start) | copy-done | bytes 1179672
  1.3 0.0 copy-start.1
  1.3 1.1 copy-done.1
  2.4 0.0 copy-start.2
  2.4 1.1 copy-done.2
  3.5 0.0 copy-start.3
  3.5 1.1 copy-done.3
  4.7 116.9 %shard_map.55 = bf16[16,4,96,128]{3,2,1,0:T(8,128)(2,1)S(1)} custom-call(bf16[128,4,1536]{2,1,0:T(4,128)(2,1)} %field_modes.1, bf16[128,4,1536]{2,1,0:T(4,128)(2,1)} %cotangent.1, bf16[768,768]{1,0:T(8,128)(2,1)S(1)} %copy-done, bf16[2,256,768]{2,1,0:T(8,128)(2,1)S(1)} %copy-done.3, bf16[2,256,768]{2,1,0:T(8,128)(2,1)S(1)} %copy-done.2, ...), custom_call_target="tpu_custom_call" | custom-call | tf_op jit(solution)/shard_map/pallas_call | solution.py:303
  121.6 1.0 copy.6
  122.6 2.5 %copy.7 = bf16[128,4,1536]{2,1,0:T(4,128)(2,1)} copy(bf16[128,4,1536]{0,2,1:T(8,128)(2,1)S(1)} %bitcast.3) | data formatting | bytes 3145728 | tf_op jit(solution)/shard_map/reshape | solution.py:331
Async XLA Ops:
  0.0 1.3 %copy-start = (bf16[768,768]{1,0:T(8,128)(2,1)S(1)}, bf16[768,768]{1,0:T(8,128)(2,1)}, u32[]{:S(2)}) copy-start(bf16[768,768]{1,0:T(8,128)(2,1)} %constant.8.clone.hartley_in) | copy-start | bytes 3538948
  1.3 1.1 copy-start.1
  2.4 1.1 copy-start.2
  3.5 1.1 copy-start.3

commit v5 on v4

--- a/solution.py
+++ b/solution.py
@@ -34,7 +34,7 @@
     field_modes, cotangent, hartley_in, lift_fields_in, lift_adjoint_in, lower_in,
     out,
     raw, hartley, lift_fields, lift_adjoint, lower, raw_sem, table_sem,
-    wide, rows, held, mixed, halves, points, total, flux, lowered, turned, result,
+    wide, rows, landed, held, mixed, halves, points, total, flux, lowered, turned, result,
     in_send, in_recv, swap_send, swap_recv, back_send, back_recv, out_send, out_recv,
 ):
     local_k, fields, columns = field_modes.shape
@@ -183,7 +183,7 @@
         target = (slot // per_share) * ncz + my_share * per_share + lax.rem(slot, per_share)
         return pltpu.make_async_remote_copy(
             src_ref=block(result.at[f], slot),
-            dst_ref=out.at[my_y, f],
+            dst_ref=landed.at[f, my_y],
             send_sem=out_send,
             recv_sem=out_recv.at[f],
             device_id=device(target),
@@ -202,7 +202,7 @@
 
         @pl.when(stays)
         def _():
-            pltpu.make_async_copy(block(result.at[f], my_slot), out.at[my_y, f], out_recv.at[f]).start()
+            pltpu.make_async_copy(block(result.at[f], my_slot), landed.at[f, my_y], out_recv.at[f]).start()
 
         @pl.when(jnp.logical_not(stays))
         def _():
@@ -257,6 +257,18 @@
     leave(2)
     finish(2)
 
+    for f in (0, 1, 3, 2):
+        wait(landed.at[f], out_recv.at[f])
+        for y in range(rows_y):
+            wide[pl.ds(y, local_m, stride=rows_y), :] = landed[f, y].astype(jnp.float32)
+
+        def turn_back(step, carry):
+            here = pl.ds(pl.multiple_of(step * chunk, chunk), chunk)
+            out[f, :, here] = wide[here, :].T.astype(jnp.bfloat16)
+            return carry
+
+        lax.fori_loop(0, columns // chunk, turn_back, 0)
+
     @pl.when(stays)
     def _():
         wait(rows.at[:, pl.ds(0, rows_y - 1)], in_send)
@@ -271,14 +283,11 @@
 
     @pl.when(stays)
     def _():
-        wait(out.at[pl.ds(0, rows_y - 1)], out_send)
+        wait(landed.at[:, pl.ds(0, rows_y - 1)], out_send)
 
     @pl.when(jnp.logical_not(stays))
     def _():
-        wait(out, out_send)
-
-    for f in range(fields):
-        wait(out.at[:, f], out_recv.at[f])
+        wait(landed, out_send)
 
 
 def on_device(nkx, ncz, field_modes, cotangent):
@@ -302,9 +311,9 @@
     dma = pltpu.SemaphoreType.DMA
     out = pl.pallas_call(
         functools.partial(kernel, nkx, ncz, shares),
-        out_shape=jax.ShapeDtypeStruct((Y, fields, local_m, local_k), bf16),
+        out_shape=jax.ShapeDtypeStruct((fields, local_k, columns), bf16),
         in_specs=[hbm] * 6,
-        out_specs=pl.BlockSpec(memory_space=pl.ANY),
+        out_specs=pl.BlockSpec(memory_space=pltpu.VMEM),
         scratch_shapes=[
             pltpu.VMEM((2, local_k, fields, columns), bf16),
             pltpu.VMEM(hartley.shape, bf16),
@@ -314,6 +323,7 @@
             dma((2,)), dma((4,)),
             pltpu.VMEM((columns, local_k), jnp.float32),
             pltpu.VMEM((2 * fields, Y, local_m, local_k), bf16),
+            pltpu.VMEM((fields, Y, local_m, local_k), bf16),
             pltpu.VMEM((2 * fields, points_x, group_k), bf16),
             pltpu.VMEM((2 * fields, points_x, group_k), bf16),
             pltpu.VMEM((2 * fields, shares, share_x, group_k), bf16),
@@ -326,9 +336,9 @@
             dma, dma((2 * fields,)), dma, dma((2 * fields,)),
             dma, dma((fields,)), dma, dma((fields,)),
         ],
-        compiler_params=pltpu.CompilerParams(has_side_effects=True, vmem_limit_bytes=48 * 2**20),
+        compiler_params=pltpu.CompilerParams(has_side_effects=True, vmem_limit_bytes=63 * 2**20),
     )(field_modes, cotangent, hartley, lift_fields, lift_adjoint, lower)
-    return out.transpose(3, 1, 2, 0).reshape(local_k, fields, columns)
+    return out.transpose(1, 0, 2)
 
 
 def solution(mesh):

time: 125 us -> 124 us (level)
  local copies, waits for them, and re-layouts: 8.15 us -> 3.77 us
  Pallas kernels: 117 us -> 120 us
    unnamed x8 -> x0, local copies, waits for them, and re-layouts: 4.67 us -> none
    pallas_call x1, Pallas kernels: 117 us -> 120 us  [on_device(): pl.pallas_call(functools.partial(kernel, nkx, ncz, shares), out_shape=jax...]
    transpose x1, local copies, waits for them, and re-layouts: 1.02 us -> 3.77 us  [on_device(): return out.transpose(1, 0, 2)]
    reshape x1 -> x0, local copies, waits for them, and re-layouts: 2.46 us -> none  [on_device(): return out.transpose(3, 1, 2, 0).reshape(local_k, fields, columns)]
where the time goes in v5:
time: 124 us
  Pallas kernels  120 us (97%)
  local copies, waits for them, and re-layouts  3.77 us (3%)
    pallas_call x1, Pallas kernels, on_device(): pl.pallas_call(functools.partial(kernel, nkx, ncz, shares), out_shape=jax...  120 us
    transpose x1, local copies, waits for them, and re-layouts, on_device(): return out.transpose(1, 0, 2)  3.77 us

profile of v5, /device:TPU:0, one launch (start us, length us, event | category | flops | bytes accessed | tf_op | source)
XLA Modules:
  0.0 124.0 jit_solution(8221288652865831712)
XLA Ops:
  0.0 120.2 %shard_map.55 = bf16[4,128,1536]{2,1,0:T(8,128)(2,1)} custom-call(bf16[128,4,1536]{2,1,0:T(4,128)(2,1)} %field_modes.1, bf16[128,4,1536]{2,1,0:T(4,128)(2,1)} %cotangent.1, bf16[768,768]{1,0:T(8,128)(2,1)} %constant.8.clone.hartley_in, bf16[2,256,768]{2,1,0:T(8,128)(2,1)} %constant.10.lift_fields_in, bf16[2,256,768]{2,1,0:T(8,128)(2,1)} %constant.12.lift_adjoint_in, ...), custom_call_target="tpu_custom_call" | custom-call | tf_op jit(solution)/shard_map/pallas_call | solution.py:312
  120.2 3.8 %copy.6 = bf16[128,4,1536]{2,1,0:T(4,128)(2,1)} copy(bf16[128,4,1536]{2,0,1:T(8,128)(2,1)} %bitcast.1) | data formatting | bytes 3145728 | tf_op jit(solution)/shard_map/transpose | solution.py:341

commit v6 on v4

--- a/solution.py
+++ b/solution.py
@@ -53,6 +53,9 @@
     stays = to_share == my_share
     far = rows_y // 2
     order = ((0, 2), (1, 0), (1, 1), (1, 3), (0, 0), (0, 1), (0, 3), (1, 2))
+    def device(target):
+        return {"kx": target // ncz, "cz": lax.rem(target, ncz)}
+
     raw_copies = [
         pltpu.make_async_copy(array, raw.at[a], raw_sem.at[a]) for a, array in enumerate((field_modes, cotangent))
     ]
@@ -69,10 +72,16 @@
     ]
     for copy in raw_copies + table_copies:
         copy.start()
+    barrier = pltpu.get_barrier_semaphore()
+
+    def greet(step, carry):
+        pl.semaphore_signal(
+            barrier, inc=1, device_id=device(lax.rem(linear + step, nkx * ncz)), device_id_type=MESH
+        )
+        return carry
+
+    lax.fori_loop(1, nkx * ncz, greet, 0)
     tables = (lift_fields, lift_adjoint)
-
-    def device(target):
-        return {"kx": target // ncz, "cz": lax.rem(target, ncz)}
 
     def block(ref, slot):
         part = lax.rem(slot, per_share)
@@ -111,6 +120,8 @@
         lax.fori_loop(0, columns // chunk, turn, 0)
         for y in range(rows_y):
             rows[h, y] = wide[pl.ds(y, local_m, stride=rows_y), :].astype(jnp.bfloat16)
+        if h == 0:
+            pl.semaphore_wait(barrier, nkx * ncz - 1)
 
         def send(step, carry):
             in_remote(h, other(my_y, step)).start()
@@ -326,7 +337,7 @@
             dma, dma((2 * fields,)), dma, dma((2 * fields,)),
             dma, dma((fields,)), dma, dma((fields,)),
         ],
-        compiler_params=pltpu.CompilerParams(has_side_effects=True, vmem_limit_bytes=48 * 2**20),
+        compiler_params=pltpu.CompilerParams(has_side_effects=True, vmem_limit_bytes=63 * 2**20, collective_id=0),
     )(field_modes, cotangent, hartley, lift_fields, lift_adjoint, lower)
     return out.transpose(3, 1, 2, 0).reshape(local_k, fields, columns)
 

time: 125 us -> 116 us (0.928)
  Pallas kernels: 117 us -> 111 us
  local copies, waits for them, and re-layouts: 8.15 us -> 4.89 us
    pallas_call x1, Pallas kernels: 117 us -> 111 us  [on_device(): pl.pallas_call(functools.partial(kernel, nkx, ncz, shares), out_shape=jax...]
    unnamed x8 -> x0, local copies, waits for them, and re-layouts: 4.67 us -> none
    transpose x1, local copies, waits for them, and re-layouts: 1.02 us -> 2.42 us  [on_device(): return out.transpose(3, 1, 2, 0).reshape(local_k, fields, columns)]
where the time goes in v6:
time: 116 us
  Pallas kernels  111 us (96%)
  local copies, waits for them, and re-layouts  4.89 us (4%)
    pallas_call x1, Pallas kernels, on_device(): pl.pallas_call(functools.partial(kernel, nkx, ncz, shares), out_shape=jax...  111 us
    reshape x1, local copies, waits for them, and re-layouts, on_device(): return out.transpose(3, 1, 2, 0).reshape(local_k, fields, columns)  2.46 us
    transpose x1, local copies, waits for them, and re-layouts, on_device(): return out.transpose(3, 1, 2, 0).reshape(local_k, fields, columns)  2.42 us

profile of v6, /device:TPU:0, one launch (start us, length us, event | category | flops | bytes accessed | tf_op | source)
XLA Modules:
  0.0 116.3 jit_solution(1519929906296791100)
XLA Ops:
  0.0 111.4 %shard_map.55 = bf16[16,4,96,128]{3,2,1,0:T(8,128)(2,1)} custom-call(bf16[128,4,1536]{2,1,0:T(4,128)(2,1)} %field_modes.1, bf16[128,4,1536]{2,1,0:T(4,128)(2,1)} %cotangent.1, bf16[768,768]{1,0:T(8,128)(2,1)} %constant.8.clone.hartley_in, bf16[2,256,768]{2,1,0:T(8,128)(2,1)} %constant.10.lift_fields_in, bf16[2,256,768]{2,1,0:T(8,128)(2,1)} %constant.12.lift_adjoint_in, ...), custom_call_target="tpu_custom_call" | custom-call | tf_op jit(solution)/shard_map/pallas_call | solution.py:314
  111.5 2.4 %copy.6 = bf16[128,4,96,16]{0,3,2,1:T(8,128)(2,1)S(1)} copy(bf16[128,4,96,16]{0,2,1,3:T(8,128)(2,1)} %bitcast.3) | data formatting | bytes 3145728 | tf_op jit(solution)/shard_map/transpose | solution.py:342
  113.9 2.5 %copy.7 = bf16[128,4,1536]{2,1,0:T(4,128)(2,1)} copy(bf16[128,4,1536]{0,2,1:T(8,128)(2,1)S(1)} %bitcast.2) | data formatting | bytes 3145728 | tf_op jit(solution)/shard_map/reshape | solution.py:342
